TPU v7x, 256 devices: a 4x2x16 block of a 4x16x16 slice. The times are simulated.
256 devices in a mesh: groups: 2 (over y), gz: 64 (over x, z), ea: 2 (over core).
Axes of the slice: x: 4, y: 2, z: 16, core: 2. Of those that a mesh axis runs over, the one named last changes fastest.
The devices are a block of a 4x16x16 slice.
Arguments:
- eigvec: bfloat16 [96, 3, 2, 128, 512], P('ea', None, None, ('groups', 'gz')), parts along dimension 3, may hold values from -3 to 3
- links: float32 [3, 3, 3, 2, 128, 512], P(None, None, None, None, ('groups', 'gz')), parts along dimension 4, may hold values from -1.8 to 1.8
- momentum: int32 [6], P('groups'), parts along dimension 0, may hold values from -2 to 2
- weights: int32 [6], P('groups'), parts along dimension 0, may hold values from 1 to 3
- spins: int32 [6, 2], P('groups'), parts along dimension 0, may hold values from 0 to 3
- peram: float32 [8, 4, 2, 96, 96], P('groups'), parts along dimension 0, may hold values from -0.4375 to 0.4375
Outputs:
- baryon_block: float32 [4, 96, 9216], P('groups', 'ea', 'gz'), parts along dimension 0
There are 2 independent parts, one for each index of `groups`. A program takes and returns all parts, laid end to end along the dimension named above; each array names one. Nothing has to cross between parts.
All inputs are finite; a program needn't handle non-finite values.
Results may differ from a plain program's by a relative error of at most 0.0045.
Values may be sent and summed in bfloat16 or wider, within the bound.
A program may use at most 64 MiB of HBM per device.

v0:
```python
import functools
import math

import jax
import jax.numpy as jnp
from jax import lax
from jax.experimental import pallas as pl
from jax.experimental.pallas import tpu as pltpu
from jax.sharding import Mesh
from jax.sharding import PartitionSpec as P

LX = 32
LY = 16
NX = 4
NZ = 16
GZ = ("gz_0", "gz_1")
GROUPS_GZ = ("groups", "gz_0", "gz_1")
MESH = pl.DeviceIdType.MESH
F32 = jnp.float32
BF16 = jnp.bfloat16
LEAD = 3


def prep_kernel(half, scale, sizes, spins, moms, p0, p1, p2, zc, mix_ref, left_ref, phase_ref):
    del spins
    ea = lax.axis_index("ea")

    def split(ref, at, value):
        high = value.astype(BF16)
        ref[0, at, :] = high
        ref[1, at, :] = (value - high.astype(F32)).astype(BF16)

    n = p0.shape[-1]
    for slot, p in ((0, p1), (1, p2)):
        re = p[0, 0, 0].T
        im = p[0, 0, 1].T
        split(mix_ref.at[slot], slice(0, n), jnp.concatenate([re, -im], 1))
        split(mix_ref.at[slot], slice(n, 2 * n), jnp.concatenate([im, re], 1))
    re = p0[0, 0, 0].T * scale
    im = p0[0, 0, 1].T * scale
    first = ea == 0
    pad = jnp.zeros((128 - 2 * half, 2 * n), F32)
    for own in range(2):
        low, high = slice(0, half), slice(half, 2 * half)
        one, two = (low, high) if own == 0 else (high, low)
        r = jnp.where(first, re[one], re[two])
        i = jnp.where(first, im[one], im[two])
        real = jnp.concatenate([r, -i], 1)
        imag = jnp.concatenate([i, r], 1)
        split(left_ref.at[0], slice(own * 128, own * 128 + 128), jnp.concatenate([real, imag, pad], 0))
        split(left_ref.at[1], slice(own * 128, own * 128 + 128), jnp.concatenate([-imag, real, pad], 0))
    lx, ly, depth = sizes
    sites = lax.broadcasted_iota(jnp.int32, (8, lx * ly), 1)
    xcoord = sites % lx
    ycoord = sites // lx
    two_pi = 2.0 * math.pi
    inplane = (moms[0] * xcoord).astype(F32) / lx + (moms[1] * ycoord).astype(F32) / ly
    along = jnp.full((8, lx * ly), moms[2] * zc[0], jnp.int32).astype(F32)
    angle = two_pi * inplane + two_pi * along / depth
    phase_ref[0] = jnp.cos(angle)
    phase_ref[1] = jnp.sin(angle)


def times(lr, li, vr, vi):
    return lr * vr - li * vi, lr * vi + li * vr


def times_conj(lr, li, vr, vi):
    return lr * vr + li * vi, lr * vi - li * vr


def main_kernel(
    weights, v_ref, links, phase, mix, left, out_ref,
    vall, upper, lower, back, disp, phown, phall, v1, v2, lmat, wbuf,
    grid_in, mine, grid_out, far_in, mid_out, x_in, zsend, zp_in, zm_in,
    halo_s, halo_r, ea_s, ea_r, dd_s, dd_r, fx_s, fx_r, x_s, x_r, zp_s, zp_r, zm_s, zm_r,
):
    ncomp, half, plane = v_ref.shape
    cols = out_ref.shape[0]
    tiles = cols // 16
    per_row = 2 * half // 16
    x = lax.axis_index("gz_0")
    z = lax.axis_index("gz_1")
    e = lax.axis_index("ea")
    nx = lax.axis_size("gz_0")
    nz = lax.axis_size("gz_1")
    sgn = 1 - 2 * e
    xp = lax.rem(x + sgn + nx, nx)
    xm = lax.rem(x - sgn + nx, nx)
    zp = lax.rem(z + 1, nz)
    zm = lax.rem(z + nz - 1, nz)
    partner = {"ea": 1 - e}
    to_xp = {"gz_0": xp}
    to_xm = {"gz_0": xm}
    to_zp = {"gz_1": zp}
    to_zm = {"gz_1": zm}
    gz = x * nz + z
    gup = lax.rem(gz + 1, nx * nz)
    gdn = lax.rem(gz + nx * nz - 1, nx * nz)
    site_up = {"gz_0": gup // nz, "gz_1": lax.rem(gup, nz)}
    site_dn = {"gz_0": gdn // nz, "gz_1": lax.rem(gdn, nz)}

    def remote(src, dst, s, r, to):
        return pltpu.make_async_remote_copy(
            src_ref=src, dst_ref=dst, send_sem=s, recv_sem=r, device_id=to, device_id_type=MESH
        )

    barrier = pltpu.get_barrier_semaphore()
    for to in (partner, to_xp, to_xm, to_zp, to_zm, site_up, site_dn):
        pl.semaphore_signal(barrier, inc=1, device_id=to, device_id_type=MESH)
    pl.semaphore_wait(barrier, 7)

    send_v = remote(v_ref, upper, halo_s.at[0], halo_r.at[0], site_dn)
    send_v.start()
    send_ea = remote(v_ref, vall.at[e], ea_s.at[0], ea_r.at[0], partner)
    send_ea.start()

    rows = 16

    def field(ref, r0):
        return [ref[c, pl.ds(r0, rows), :].astype(F32) for c in range(ncomp)]

    def link(d, row, col, part):
        return links[pl.ds(((d * 3 + row) * 3 + col) * 2 + part, 1), :]

    def apply(d, f):
        out = []
        for row in range(3):
            re, im = 0.0, 0.0
            for col in range(3):
                a, b = times(link(d, row, col, 0), link(d, row, col, 1), f[2 * col], f[2 * col + 1])
                re, im = re + a, im + b
            out += [re, im]
        return out

    def adjoint(d, f):
        out = []
        for col in range(3):
            re, im = 0.0, 0.0
            for row in range(3):
                a, b = times_conj(
                    link(d, row, col, 0), link(d, row, col, 1), f[2 * row], f[2 * row + 1]
                )
                re, im = re + a, im + b
            out += [re, im]
        return out

    def back_tile(t, _):
        r0 = pl.multiple_of(t * rows, rows)
        f = field(v_ref, r0)
        for c, val in enumerate(adjoint(2, f)):
            back[c, pl.ds(r0, rows), :] = val.astype(BF16)
        for c in range(ncomp):
            vall[e, c, pl.ds(r0, rows), :] = v_ref[c, pl.ds(r0, rows), :]
        return 0

    lax.fori_loop(0, half // rows, back_tile, 0)
    send_b = remote(back, lower, halo_s.at[1], halo_r.at[1], site_up)
    send_b.start()

    lane = lax.broadcasted_iota(jnp.int32, (rows, plane), 1)
    xc = lax.rem(lane, LX)

    def shift_x(val, by):
        if by < 0:
            return jnp.where(
                xc == LX - 1, pltpu.roll(val, LX - 1, 1), pltpu.roll(val, plane - 1, 1)
            )
        return jnp.where(xc == 0, pltpu.roll(val, plane - (LX - 1), 1), pltpu.roll(val, 1, 1))

    def shift_y(val, by):
        return pltpu.roll(val, plane - LX if by < 0 else LX, 1)

    def inplane_tile(t, _):
        r0 = pl.multiple_of(t * rows, rows)
        for d, shift in ((0, shift_x), (1, shift_y)):
            f = field(v_ref, r0)
            ahead = apply(d, [shift(c, -1) for c in f])
            behind = [shift(c.astype(BF16).astype(F32), 1) for c in adjoint(d, f)]
            for c in range(ncomp):
                term = weights[d].astype(F32) * (ahead[c] - behind[c])
                if d == 0:
                    disp[c, pl.ds(r0, rows), :] = term
                else:
                    disp[c, pl.ds(r0, rows), :] += term
        return 0

    lax.fori_loop(0, half // rows, inplane_tile, 0)

    send_ea.wait()
    for slot, dst in ((0, v1), (1, v2)):
        for k in range(3):
            stack = jnp.concatenate(
                [vall[0, 2 * k], vall[1, 2 * k], vall[0, 2 * k + 1], vall[1, 2 * k + 1]], 0
            )
            res = jnp.dot(mix[slot, 0], stack, preferred_element_type=F32) + jnp.dot(
                mix[slot, 1], stack, preferred_element_type=F32
            )
            for r in range(2):
                part = res[2 * half * r : 2 * half * (r + 1)]
                for lt in range(plane // 128):
                    dst[2 * k + r, lt] = part[:, lt * 128 : lt * 128 + 128]

    send_v.wait()
    send_b.wait()
    cosine = phase[0, 0:1]
    sine = phase[1, 0:1]

    def zdir_tile(t, _):
        r0 = pl.multiple_of(t * rows, rows)
        ahead = apply(2, field(upper, r0))
        low = field(lower, r0)
        tot = [
            disp[c, pl.ds(r0, rows), :] + weights[2].astype(F32) * (ahead[c] - low[c])
            for c in range(ncomp)
        ]
        for k in range(3):
            re, im = tot[2 * k], tot[2 * k + 1]
            phown[2 * k, pl.ds(r0, rows), :] = (cosine * re + sine * im).astype(BF16)
            phown[2 * k + 1, pl.ds(r0, rows), :] = (cosine * im - sine * re).astype(BF16)
        for c in range(ncomp):
            phall[e, c, pl.ds(r0, rows), :] = phown[c, pl.ds(r0, rows), :]
        return 0

    lax.fori_loop(0, half // rows, zdir_tile, 0)
    send_ph = remote(phown, phall.at[e], ea_s.at[1], ea_r.at[1], partner)
    send_ph.start()
    send_ph.wait()
    for k in range(3):
        stack = jnp.concatenate(
            [phall[0, 2 * k], phall[1, 2 * k], phall[0, 2 * k + 1], phall[1, 2 * k + 1]], 0
        )
        for r in range(2):
            res = jnp.dot(left[r, 0], stack, preferred_element_type=F32) + jnp.dot(
                left[r, 1], stack, preferred_element_type=F32
            )
            lmat[pl.ds((2 * k + r) * plane, plane), :] = res.T.astype(BF16)

    def dest_z(q):
        step = q // 2
        return lax.rem(jnp.where(lax.rem(q, 2) == 0, z + 8 - step, z - 7 + step) + nz, nz)

    def w_tile(t, zd, blk):
        xd = lax.rem(jnp.where(blk == 0, x + sgn + nx, x + 2 * (1 - e)), nx)
        at = (xd * nz + zd) * tiles + t
        b2 = at // per_row
        c0 = pl.multiple_of(lax.rem(at, per_row) * 16, 16)
        row0 = pl.multiple_of(t * 16, 16)
        for lt in range(plane // 128):
            b = [v1[c, lt, pl.ds(b2, 16, stride=0), :] for c in range(ncomp)]
            w = [v2[c, lt, pl.ds(c0, 16), :] for c in range(ncomp)]
            for k, (i, j) in enumerate(((1, 2), (2, 0), (0, 1))):
                ar, ai, br, bi = b[2 * i], b[2 * i + 1], b[2 * j], b[2 * j + 1]
                cr, ci, dr, di = w[2 * i], w[2 * i + 1], w[2 * j], w[2 * j + 1]
                re = ar * dr - ai * di - (br * cr - bi * ci)
                im = ar * di + ai * dr - (br * ci + bi * cr)
                at_re = (2 * k) * plane + lt * 128
                at_im = (2 * k + 1) * plane + lt * 128
                wbuf[pl.ds(row0, 16), at_re : at_re + 128] = re.astype(BF16)
                wbuf[pl.ds(row0, 16), at_im : at_im + 128] = im.astype(BF16)

    def to_partner(q, blk):
        role = 1 if blk == 0 else 2 + e
        return remote(
            grid_out.at[q, blk], grid_in.at[q, role], dd_s.at[q, blk], dd_r.at[q, blk], partner
        )

    def compute(q):
        zd = dest_z(q)
        for blk in range(2):
            lax.fori_loop(0, tiles, lambda t, c: (w_tile(t, zd, blk), 0)[1], 0)
            res = jnp.dot(wbuf[...], lmat[...], preferred_element_type=F32)
            grid_out[q, blk] = res[:, 128:].astype(BF16)
            to_partner(q, blk).start()
            mine[q, blk] = res[:, :128].astype(BF16)

    def far_copy(q):
        return remote(grid_in.at[q, 2], far_in.at[q], fx_s.at[q], fx_r.at[q], to_xp)

    def far_mine(q):
        return remote(mine.at[q, 1], far_in.at[q], fx_s.at[q], fx_r.at[q], to_xp)

    def direct_copy(q):
        return remote(grid_in.at[q, 1], x_in.at[q, 0], x_s.at[q, 0], x_r.at[q, 0], to_xm)

    def mid_copy(q):
        return remote(mid_out.at[q], x_in.at[q, 1], x_s.at[q, 1], x_r.at[q, 1], to_xp)

    def first_x(q):
        to_partner(q, 0).wait_recv()
        to_partner(q, 1).wait_recv()

        @pl.when(e == 0)
        def _():
            far_mine(q).start()

        @pl.when(e == 1)
        def _():
            far_copy(q).start()

        direct_copy(q).start()

    def second_x(q):
        far_mine(q).wait_recv()
        mid_out[q] = (mine[q, 0].astype(F32) + far_in[q].astype(F32)).astype(BF16)
        mid_copy(q).start()

    def x_sum(q):
        direct_copy(q).wait_recv()
        mid_copy(q).wait_recv()
        total = x_in[q, 0].astype(F32) + x_in[q, 1].astype(F32)
        own = jnp.where(e == 0, grid_in[q, 3].astype(F32), mine[q, 1].astype(F32))
        return total + own

    def plus_copy(step):
        return remote(zsend.at[0, step], zp_in.at[step], zp_s.at[step], zp_r.at[step], to_zp)

    def minus_copy(step):
        return remote(zsend.at[1, step], zm_in.at[step], zm_s.at[step], zm_r.at[step], to_zm)

    last = 7

    def ring(step):
        zsend[0, step] = x_sum(2 * step)
        zsend[1, step] = x_sum(2 * step + 1)

        @pl.when(step > 0)
        def _():
            plus_copy(step - 1).wait_recv()
            zsend[0, step] += zp_in[step - 1]

        plus_copy(step).start()

        @pl.when(step > 0)
        def _():
            minus_copy(step - 1).wait_recv()
            zsend[1, step] += zm_in[step - 1]

        @pl.when(step < last)
        def _():
            minus_copy(step).start()

    def body(i, _):
        @pl.when(i <= last)
        def _():
            compute(2 * i)
            compute(2 * i + 1)

        @pl.when((i >= 1) & (i <= last + 1))
        def _():
            first_x(2 * (i - 1))
            first_x(2 * (i - 1) + 1)

        @pl.when((i >= 2) & (i <= last + 2))
        def _():
            second_x(2 * (i - 2))
            second_x(2 * (i - 2) + 1)

        @pl.when(i >= 3)
        def _():
            ring(i - 3)

        return 0

    lax.fori_loop(0, last + 4, body, 0)
    plus_copy(last).wait_recv()
    out_ref[...] = zsend[1, last] + zp_in[last]

    def drain(q, _):
        to_partner(q, 0).wait_send()
        to_partner(q, 1).wait_send()
        far_mine(q).wait_send()
        direct_copy(q).wait_send()
        mid_copy(q).wait_send()
        return 0

    lax.fori_loop(0, 2 * (last + 1), drain, 0)
    for step in range(last + 1):
        plus_copy(step).wait_send()
        if step < last:
            minus_copy(step).wait_send()


def shards(eigvec, links, momentum, weights, spins, peram):
    half = eigvec.shape[0]
    plane = eigvec.shape[4]
    n = 2 * half
    nx, nz, cores = lax.axis_size("gz_0"), lax.axis_size("gz_1"), lax.axis_size("ea")
    depth = nx * nz
    cols = n * n // depth
    scale = 1.0 / math.sqrt(LX * LY * depth)
    zcoord = lax.axis_index(GZ).astype(jnp.int32).reshape(1)

    def block_of(q):
        return pl.BlockSpec((1, 1, 2, n, n), lambda i, sp, mo: (sp[q, 0], sp[q, 1], 0, 0, 0))

    mix, left, phase = pl.pallas_call(
        functools.partial(prep_kernel, half, scale, (LX, LY, depth)),
        grid_spec=pltpu.PrefetchScalarGridSpec(
            num_scalar_prefetch=2,
            grid=(1,),
            in_specs=[block_of(0), block_of(1), block_of(2), pl.BlockSpec(memory_space=pltpu.SMEM)],
            out_specs=[
                pl.BlockSpec((2, 2, 2 * n, 2 * n), lambda i, sp, mo: (0, 0, 0, 0)),
                pl.BlockSpec((2, 2, 256, 2 * n), lambda i, sp, mo: (0, 0, 0, 0)),
                pl.BlockSpec((2, 8, plane), lambda i, sp, mo: (0, 0, 0)),
            ],
        ),
        out_shape=[
            jax.ShapeDtypeStruct((2, 2, 2 * n, 2 * n), BF16),
            jax.ShapeDtypeStruct((2, 2, 256, 2 * n), BF16),
            jax.ShapeDtypeStruct((2, 8, plane), F32),
        ],
    )(spins, momentum, peram, peram, peram, zcoord)

    fields = eigvec.reshape(half, 6, plane).transpose(1, 0, 2)
    link_rows = links.reshape(54, plane)
    vm = pl.BlockSpec(memory_space=pltpu.VMEM)
    dma = pltpu.SemaphoreType.DMA
    nq = nz
    out = pl.pallas_call(
        main_kernel,
        out_shape=jax.ShapeDtypeStruct((cols, 128), F32),
        in_specs=[pl.BlockSpec(memory_space=pltpu.SMEM)] + [vm] * 5,
        out_specs=vm,
        scratch_shapes=[
            pltpu.VMEM((2, 6, half, plane), BF16),
            pltpu.VMEM((6, half, plane), BF16),
            pltpu.VMEM((6, half, plane), BF16),
            pltpu.VMEM((6, half, plane), BF16),
            pltpu.VMEM((6, half, plane), F32),
            pltpu.VMEM((6, half, plane), BF16),
            pltpu.VMEM((2, 6, half, plane), BF16),
            pltpu.VMEM((6, plane // 128, n, 128), F32),
            pltpu.VMEM((6, plane // 128, n, 128), F32),
            pltpu.VMEM((6 * plane, 256), BF16),
            pltpu.VMEM((cols, 6 * plane), BF16),
            pltpu.VMEM((nq, 4, cols, 128), BF16),
            pltpu.VMEM((nq, 2, cols, 128), BF16),
            pltpu.VMEM((nq, 2, cols, 128), BF16),
            pltpu.VMEM((nq, cols, 128), BF16),
            pltpu.VMEM((nq, cols, 128), BF16),
            pltpu.VMEM((nq, 2, cols, 128), BF16),
            pltpu.VMEM((2, 8, cols, 128), F32),
            pltpu.VMEM((8, cols, 128), F32),
            pltpu.VMEM((8, cols, 128), F32),
            dma((2,)), dma((2,)), dma((2,)), dma((2,)),
            dma((nq, 2)), dma((nq, 2)), dma((nq,)), dma((nq,)),
            dma((nq, 2)), dma((nq, 2)), dma((8,)), dma((8,)), dma((8,)), dma((8,)),
        ],
        compiler_params=pltpu.CompilerParams(
            collective_id=0, has_side_effects=True, vmem_limit_bytes=60 * 1024 * 1024
        ),
    )(weights, fields, link_rows, phase, mix, left)
    return out[:, :n].reshape(cols, 2, half).transpose(1, 2, 0)


def solution(mesh):
    split = Mesh(
        mesh.devices.reshape(mesh.shape["groups"], NX, NZ, mesh.shape["ea"]),
        ("groups", "gz_0", "gz_1", "ea"),
    )
    in_specs = (
        P("ea", None, None, GROUPS_GZ, None),
        P(None, None, None, None, GROUPS_GZ, None),
        P("groups"),
        P("groups"),
        P("groups", None),
        P("groups", None, None, None, None),
    )
    out_specs = P("groups", "ea", GZ)
    return jax.shard_map(
        shards, mesh=split, in_specs=in_specs, out_specs=out_specs, check_vma=False
    )
```

profile of v0, /device:TPU:40, one launch (start us, length us, event | category | flops | bytes accessed | tf_op | source)
XLA Modules:
  0.0 105.8 jit_solution(4871115713661251283)
XLA Ops:
  0.0 1.3 %copy.11.spins = s32[3,2]{1,0:T(4,128)} copy(s32[3,2]{0,1:T(2,128)} %param.10) | data formatting | bytes 48 | tf_op args[4]
  1.3 1.2 %reduce = f32[3,3,3,2,512]{4,3,2,1,0:T(2,128)S(1)} reduce(f32[3,3,3,2,1,512]{5,4,3,2,1,0:T(1,128)} %param.7, f32[]{:T(128)} %constant.19), dimensions={4}, to_apply=%param.7.reduce_sub_computation | reduce | bytes 221188 | tf_op args[1]
  2.6 0.7 reshape.13.links
  3.3 1.7 %copy.10 = bf16[48,3,2,1,512]{4,0,2,1,3:T(8,128)(2,1)} copy(bf16[48,3,2,1,512]{4,2,3,1,0:T(2,128)(2,1)} %param.6) | data formatting | bytes 589824 | tf_op args[0]
  5.0 2.9 %shard_map.64 = (bf16[2,2,192,192]{3,2,1,0:T(8,128)(2,1)}, bf16[2,2,256,192]{3,2,1,0:T(8,128)(2,1)}, f32[2,8,512]{2,1,0:T(8,128)}) custom-call(s32[3,2]{1,0:T(4,128)} %copy.11.spins, s32[3]{0:T(128)} %moms.1, f32[4,4,2,96,96]{4,3,2,1,0:T(8,128)} %p2.1, f32[4,4,2,96,96]{4,3,2,1,0:T(8,128)} %p2.1, f32[4,4,2,96,96]{4,3,2,1,0:T(8,128)} %p2.1, s32[1]{0:T(128)} %bitcast.2.zc), custom_call_target="tpu_custom_call" | custom-call | tf_op jit(solution)/shard_map/pallas_call | solution.py:397
  7.9 96.3 %shard_map.65 = f32[144,128]{1,0:T(8,128)} custom-call(s32[3]{0:T(128)} %weights.1, bf16[6,48,512]{2,1,0:T(8,128)(2,1)} %bitcast.8, f32[54,512]{1,0:T(8,128)} %reshape.13.links, f32[2,8,512]{2,1,0:T(8,128)} %get-tuple-element.8.phase, bf16[2,2,192,192]{3,2,1,0:T(8,128)(2,1)} %get-tuple-element.9.mix, bf16[2,2,256,192]{3,2,1,0:T(8,128)(2,1)} %get-tuple-element.10.left), custom_call_target="tpu_custom_call" | custom-call | tf_op jit(solution)/shard_map/pallas_call | solution.py:421
  104.2 1.6 %copy.12 = f32[144,96]{0,1:T(8,128)} copy(f32[144,96]{1,0:T(8,128)} %bitcast.9) | data formatting | bytes 110592 | tf_op jit(solution)/shard_map/slice | solution.py:455
where the time goes:
time: 106 us
  Pallas kernels  99.2 us (94%)
  local copies, waits for them, and re-layouts  5.39 us (5%)
  other arithmetic  1.22 us (1%)
    pallas_call x1, Pallas kernels, shards(): pl.pallas_call(main_kernel, out_shape=jax.ShapeDtypeStruct((cols, 128), F...  96.3 us
    unnamed x2, local copies, waits for them, and re-layouts  3.04 us
    pallas_call x1, Pallas kernels, shards(): pl.pallas_call(functools.partial(prep_kernel, half, scale, (LX, LY, depth...  2.87 us

commit v1 on v0

--- a/solution.py
+++ b/solution.py
@@ -13,12 +13,12 @@
 LY = 16
 NX = 4
 NZ = 16
+SIDE = 4
 GZ = ("gz_0", "gz_1")
 GROUPS_GZ = ("groups", "gz_0", "gz_1")
 MESH = pl.DeviceIdType.MESH
 F32 = jnp.float32
 BF16 = jnp.bfloat16
-LEAD = 3
 
 
 def prep_kernel(half, scale, sizes, spins, moms, p0, p1, p2, zc, mix_ref, left_ref, phase_ref):
@@ -71,12 +71,13 @@
 
 def main_kernel(
     weights, v_ref, links, phase, mix, left, out_ref,
-    vall, upper, lower, back, disp, phown, phall, v1, v2, lmat, wbuf,
-    grid_in, mine, grid_out, far_in, mid_out, x_in, zsend, zp_in, zm_in,
-    halo_s, halo_r, ea_s, ea_r, dd_s, dd_r, fx_s, fx_r, x_s, x_r, zp_s, zp_r, zm_s, zm_r,
+    vall, upper, lower, back, disp, phown, phall, v1, v2, lmat, wbuf0, wbuf1, acc,
+    grid_in, mine, grid_out, far_in, mid_out, x_in, near_out, near_in, near_own, long_out, long_in,
+    halo_s, halo_r, ea_s, ea_r, dd_s, dd_r, fx_s, fx_r, x_s, x_r, near_s, near_r, long_s, long_r,
 ):
     ncomp, half, plane = v_ref.shape
     cols = out_ref.shape[0]
+    packed = far_in.shape[1]
     tiles = cols // 16
     per_row = 2 * half // 16
     x = lax.axis_index("gz_0")
@@ -87,28 +88,39 @@
     sgn = 1 - 2 * e
     xp = lax.rem(x + sgn + nx, nx)
     xm = lax.rem(x - sgn + nx, nx)
-    zp = lax.rem(z + 1, nz)
-    zm = lax.rem(z + nz - 1, nz)
+    zh = z // SIDE
+    zl = lax.rem(z, SIDE)
     partner = {"ea": 1 - e}
     to_xp = {"gz_0": xp}
     to_xm = {"gz_0": xm}
-    to_zp = {"gz_1": zp}
-    to_zm = {"gz_1": zm}
     gz = x * nz + z
     gup = lax.rem(gz + 1, nx * nz)
     gdn = lax.rem(gz + nx * nz - 1, nx * nz)
     site_up = {"gz_0": gup // nz, "gz_1": lax.rem(gup, nz)}
     site_dn = {"gz_0": gdn // nz, "gz_1": lax.rem(gdn, nz)}
 
+    def in_side(r):
+        return {"gz_1": zh * SIDE + lax.rem(zl + r, SIDE)}
+
+    def across(r):
+        return {"gz_1": lax.rem(zh + r, SIDE) * SIDE + zl}
+
+    def turn_of(n):
+        return jnp.where(n == 0, 2, jnp.where(n == 1, 1, jnp.where(n == 2, 3, 0)))
+
     def remote(src, dst, s, r, to):
         return pltpu.make_async_remote_copy(
             src_ref=src, dst_ref=dst, send_sem=s, recv_sem=r, device_id=to, device_id_type=MESH
         )
 
     barrier = pltpu.get_barrier_semaphore()
-    for to in (partner, to_xp, to_xm, to_zp, to_zm, site_up, site_dn):
+    peers = [partner, to_xp, to_xm, site_up, site_dn]
+    for r in range(1, SIDE):
+        peers.append(in_side(r))
+        peers.append(across(r))
+    for to in peers:
         pl.semaphore_signal(barrier, inc=1, device_id=to, device_id_type=MESH)
-    pl.semaphore_wait(barrier, 7)
+    pl.semaphore_wait(barrier, len(peers))
 
     send_v = remote(v_ref, upper, halo_s.at[0], halo_r.at[0], site_dn)
     send_v.start()
@@ -121,7 +133,7 @@
         return [ref[c, pl.ds(r0, rows), :].astype(F32) for c in range(ncomp)]
 
     def link(d, row, col, part):
-        return links[pl.ds(((d * 3 + row) * 3 + col) * 2 + part, 1), :]
+        return links[((d * 3 + row) * 3 + col) * 2 + part]
 
     def apply(d, f):
         out = []
@@ -185,8 +197,6 @@
                     disp[c, pl.ds(r0, rows), :] += term
         return 0
 
-    lax.fori_loop(0, half // rows, inplane_tile, 0)
-
     send_ea.wait()
     for slot, dst in ((0, v1), (1, v2)):
         for k in range(3):
@@ -201,6 +211,170 @@
                 for lt in range(plane // 128):
                     dst[2 * k + r, lt] = part[:, lt * 128 : lt * 128 + 128]
 
+    def dest_z(q):
+        hop = lax.rem(zh + turn_of(q // SIDE), SIDE)
+        return hop * SIDE + lax.rem(zl + turn_of(lax.rem(q, SIDE)), SIDE)
+
+    turns = 4
+
+    def w_section(dst, step, sec):
+        par = sec // 2
+        blk = sec - 2 * par
+        xd = lax.rem(jnp.where(blk == 0, x + sgn + nx, x + 2 * (1 - e)), nx)
+        first = (xd * nz + dest_z(2 * step + par)) * tiles
+        row = first // per_row
+        skip = first - row * per_row
+        for t in range(tiles):
+            u = skip + t
+            over = jnp.where(u >= per_row, 1, 0) + jnp.where(u >= 2 * per_row, 1, 0)
+            b2 = row + over
+            c0 = pl.multiple_of((u - over * per_row) * 16, 16)
+            row0 = pl.multiple_of(sec * cols + t * 16, 16)
+            for lt in range(plane // 128):
+                b = [v1[c, lt, pl.ds(b2, 16, stride=0), :] for c in range(ncomp)]
+                w = [v2[c, lt, pl.ds(c0, 16), :] for c in range(ncomp)]
+                for k, (i, j) in enumerate(((1, 2), (2, 0), (0, 1))):
+                    ar, ai, br, bi = b[2 * i], b[2 * i + 1], b[2 * j], b[2 * j + 1]
+                    cr, ci, dr, di = w[2 * i], w[2 * i + 1], w[2 * j], w[2 * j + 1]
+                    re = ar * dr - ai * di - (br * cr - bi * ci)
+                    im = ar * di + ai * dr - (br * ci + bi * cr)
+                    for r, val in ((0, re), (1, im)):
+                        piece = 2 * (2 * k + r) + lt // 2
+                        at = (piece % 3) * 256 + (lt % 2) * 128
+                        dst[piece // 3, pl.ds(row0, 16), at : at + 128] = val.astype(BF16)
+
+    def w_only(dst, step):
+        lax.fori_loop(0, turns, lambda k, c: (w_section(dst, step, k), 0)[1], 0)
+
+    def dot_turn(src, k):
+        acc[...] += jnp.dot(src[k], lmat[k], preferred_element_type=F32)
+
+    def fused(src, dst, step):
+        acc[...] = jnp.zeros_like(acc)
+
+        def turn(k, _):
+            dot_turn(src, k)
+            w_section(dst, step + 1, k)
+            return 0
+
+        lax.fori_loop(0, turns, turn, 0)
+
+    def dot_only(src):
+        acc[...] = jnp.zeros_like(acc)
+        lax.fori_loop(0, turns, lambda k, c: (dot_turn(src, k), 0)[1], 0)
+
+    def to_partner(q, blk):
+        role = 1 if blk == 0 else 2 + e
+        return remote(
+            grid_out.at[q, blk], grid_in.at[q, role], dd_s.at[q, blk], dd_r.at[q, blk], partner
+        )
+
+    fill = lax.broadcasted_iota(jnp.int32, (32, 128), 1) < 2 * half
+
+    def pack(rows_at, lanes):
+        for g in range(3):
+            extra = acc[rows_at + packed : rows_at + cols, lanes]
+            extra = pltpu.roll(extra, 2 * half - 32 * g, 1)
+            yield jnp.where(fill, acc[rows_at + 32 * g : rows_at + 32 * g + 32, lanes], extra)
+        yield acc[rows_at + 96 : rows_at + packed, lanes]
+
+    def put(ref, pieces):
+        at = 0
+        for piece in pieces:
+            ref[at : at + piece.shape[0], :] = piece.astype(BF16)
+            at += piece.shape[0]
+
+    def give(step):
+        for par in range(2):
+            for blk in range(2):
+                q = 2 * step + par
+                rows_at = (2 * par + blk) * cols
+                put(grid_out.at[q, blk], pack(rows_at, slice(128, 256)))
+                to_partner(q, blk).start()
+                put(mine.at[q, blk], pack(rows_at, slice(0, 128)))
+
+    def far_copy(q):
+        return remote(grid_in.at[q, 2], far_in.at[q], fx_s.at[q], fx_r.at[q], to_xp)
+
+    def far_mine(q):
+        return remote(mine.at[q, 1], far_in.at[q], fx_s.at[q], fx_r.at[q], to_xp)
+
+    def direct_copy(q):
+        return remote(grid_in.at[q, 1], x_in.at[q, 0], x_s.at[q, 0], x_r.at[q, 0], to_xm)
+
+    def mid_copy(q):
+        return remote(mid_out.at[q], x_in.at[q, 1], x_s.at[q, 1], x_r.at[q, 1], to_xp)
+
+    def first_x(q):
+        to_partner(q, 0).wait_recv()
+        to_partner(q, 1).wait_recv()
+
+        @pl.when(e == 0)
+        def _():
+            far_mine(q).start()
+
+        @pl.when(e == 1)
+        def _():
+            far_copy(q).start()
+
+        direct_copy(q).start()
+
+    def second_x(q):
+        far_mine(q).wait_recv()
+        mid_out[q] = (mine[q, 0].astype(F32) + far_in[q].astype(F32)).astype(BF16)
+        mid_copy(q).start()
+
+    def x_sum(q):
+        direct_copy(q).wait_recv()
+        mid_copy(q).wait_recv()
+        total = x_in[q, 0].astype(F32) + x_in[q, 1].astype(F32)
+        own = jnp.where(e == 0, grid_in[q, 3].astype(F32), mine[q, 1].astype(F32))
+        return total + own
+
+    last = 7
+
+    def near_copy(q, g, r):
+        return remote(near_out.at[q], near_in.at[g, r], near_s.at[q], near_r.at[g, r], in_side(r))
+
+    def near_sum(step):
+        for par in range(2):
+            q = 2 * step + par
+            g = q // SIDE
+            r = turn_of(lax.rem(q, SIDE))
+            total = x_sum(q)
+            if par == 0:
+                near_out[q] = total.astype(BF16)
+                near_copy(q, g, r).start()
+            else:
+
+                @pl.when(r > 0)
+                def _():
+                    near_out[q] = total.astype(BF16)
+                    near_copy(q, g, r).start()
+
+                @pl.when(r == 0)
+                def _():
+                    near_own[g] = total
+
+    def long_copy(g):
+        return remote(
+            long_out.at[g], long_in.at[g], long_s.at[g], long_r.at[g], across(turn_of(g))
+        )
+
+    def long_sum(g):
+        total = near_own[g]
+        for r in range(1, SIDE):
+            near_copy(0, g, r).wait_recv()
+            total = total + near_in[g, r].astype(F32)
+        near_own[g] = total
+
+        @pl.when(g < SIDE - 1)
+        def _():
+            long_out[g] = near_own[g]
+            long_copy(g).start()
+
+    w_only(wbuf0, 0)
+    lax.fori_loop(0, half // rows, inplane_tile, 0)
     send_v.wait()
     send_b.wait()
     cosine = phase[0, 0:1]
@@ -234,137 +408,62 @@
             res = jnp.dot(left[r, 0], stack, preferred_element_type=F32) + jnp.dot(
                 left[r, 1], stack, preferred_element_type=F32
             )
-            lmat[pl.ds((2 * k + r) * plane, plane), :] = res.T.astype(BF16)
-
-    def dest_z(q):
-        step = q // 2
-        return lax.rem(jnp.where(lax.rem(q, 2) == 0, z + 8 - step, z - 7 + step) + nz, nz)
-
-    def w_tile(t, zd, blk):
-        xd = lax.rem(jnp.where(blk == 0, x + sgn + nx, x + 2 * (1 - e)), nx)
-        at = (xd * nz + zd) * tiles + t
-        b2 = at // per_row
-        c0 = pl.multiple_of(lax.rem(at, per_row) * 16, 16)
-        row0 = pl.multiple_of(t * 16, 16)
-        for lt in range(plane // 128):
-            b = [v1[c, lt, pl.ds(b2, 16, stride=0), :] for c in range(ncomp)]
-            w = [v2[c, lt, pl.ds(c0, 16), :] for c in range(ncomp)]
-            for k, (i, j) in enumerate(((1, 2), (2, 0), (0, 1))):
-                ar, ai, br, bi = b[2 * i], b[2 * i + 1], b[2 * j], b[2 * j + 1]
-                cr, ci, dr, di = w[2 * i], w[2 * i + 1], w[2 * j], w[2 * j + 1]
-                re = ar * dr - ai * di - (br * cr - bi * ci)
-                im = ar * di + ai * dr - (br * ci + bi * cr)
-                at_re = (2 * k) * plane + lt * 128
-                at_im = (2 * k + 1) * plane + lt * 128
-                wbuf[pl.ds(row0, 16), at_re : at_re + 128] = re.astype(BF16)
-                wbuf[pl.ds(row0, 16), at_im : at_im + 128] = im.astype(BF16)
-
-    def to_partner(q, blk):
-        role = 1 if blk == 0 else 2 + e
-        return remote(
-            grid_out.at[q, blk], grid_in.at[q, role], dd_s.at[q, blk], dd_r.at[q, blk], partner
-        )
-
-    def compute(q):
-        zd = dest_z(q)
-        for blk in range(2):
-            lax.fori_loop(0, tiles, lambda t, c: (w_tile(t, zd, blk), 0)[1], 0)
-            res = jnp.dot(wbuf[...], lmat[...], preferred_element_type=F32)
-            grid_out[q, blk] = res[:, 128:].astype(BF16)
-            to_partner(q, blk).start()
-            mine[q, blk] = res[:, :128].astype(BF16)
-
-    def far_copy(q):
-        return remote(grid_in.at[q, 2], far_in.at[q], fx_s.at[q], fx_r.at[q], to_xp)
-
-    def far_mine(q):
-        return remote(mine.at[q, 1], far_in.at[q], fx_s.at[q], fx_r.at[q], to_xp)
-
-    def direct_copy(q):
-        return remote(grid_in.at[q, 1], x_in.at[q, 0], x_s.at[q, 0], x_r.at[q, 0], to_xm)
-
-    def mid_copy(q):
-        return remote(mid_out.at[q], x_in.at[q, 1], x_s.at[q, 1], x_r.at[q, 1], to_xp)
-
-    def first_x(q):
-        to_partner(q, 0).wait_recv()
-        to_partner(q, 1).wait_recv()
-
-        @pl.when(e == 0)
-        def _():
-            far_mine(q).start()
-
-        @pl.when(e == 1)
-        def _():
-            far_copy(q).start()
-
-        direct_copy(q).start()
-
-    def second_x(q):
-        far_mine(q).wait_recv()
-        mid_out[q] = (mine[q, 0].astype(F32) + far_in[q].astype(F32)).astype(BF16)
-        mid_copy(q).start()
-
-    def x_sum(q):
-        direct_copy(q).wait_recv()
-        mid_copy(q).wait_recv()
-        total = x_in[q, 0].astype(F32) + x_in[q, 1].astype(F32)
-        own = jnp.where(e == 0, grid_in[q, 3].astype(F32), mine[q, 1].astype(F32))
-        return total + own
-
-    def plus_copy(step):
-        return remote(zsend.at[0, step], zp_in.at[step], zp_s.at[step], zp_r.at[step], to_zp)
-
-    def minus_copy(step):
-        return remote(zsend.at[1, step], zm_in.at[step], zm_s.at[step], zm_r.at[step], to_zm)
-
-    last = 7
-
-    def ring(step):
-        zsend[0, step] = x_sum(2 * step)
-        zsend[1, step] = x_sum(2 * step + 1)
-
-        @pl.when(step > 0)
-        def _():
-            plus_copy(step - 1).wait_recv()
-            zsend[0, step] += zp_in[step - 1]
-
-        plus_copy(step).start()
-
-        @pl.when(step > 0)
-        def _():
-            minus_copy(step - 1).wait_recv()
-            zsend[1, step] += zm_in[step - 1]
-
+            turned = res.T.astype(BF16)
+            for hf in range(2):
+                piece = 2 * (2 * k + r) + hf
+                at = (piece % 3) * 256
+                lmat[piece // 3, at : at + 256, :] = turned[hf * 256 : hf * 256 + 256]
+
+    def stage(step, src, dst):
         @pl.when(step < last)
         def _():
-            minus_copy(step).start()
+            fused(src, dst, step)
+
+        @pl.when(step == last)
+        def _():
+            dot_only(src)
+
+        @pl.when((step >= 1) & (step <= last + 1))
+        def _():
+            first_x(2 * (step - 1))
+            first_x(2 * (step - 1) + 1)
+
+        @pl.when(step <= last)
+        def _():
+            give(step)
+
+        @pl.when((step >= 3) & (step <= last + 3))
+        def _():
+            second_x(2 * (step - 3))
+            second_x(2 * (step - 3) + 1)
+
+        @pl.when((step >= 5) & (step <= last + 5))
+        def _():
+            near_sum(step - 5)
 
     def body(i, _):
-        @pl.when(i <= last)
-        def _():
-            compute(2 * i)
-            compute(2 * i + 1)
-
-        @pl.when((i >= 1) & (i <= last + 1))
-        def _():
-            first_x(2 * (i - 1))
-            first_x(2 * (i - 1) + 1)
-
-        @pl.when((i >= 2) & (i <= last + 2))
-        def _():
-            second_x(2 * (i - 2))
-            second_x(2 * (i - 2) + 1)
+        stage(2 * i, wbuf0, wbuf1)
+
+        stage(2 * i + 1, wbuf1, wbuf0)
 
         @pl.when(i >= 3)
         def _():
-            ring(i - 3)
+            long_sum(i - 3)
 
         return 0
 
-    lax.fori_loop(0, last + 4, body, 0)
-    plus_copy(last).wait_recv()
-    out_ref[...] = zsend[1, last] + zp_in[last]
+    lax.fori_loop(0, 7, body, 0)
+    total = near_own[SIDE - 1]
+    for g in range(SIDE - 1):
+        long_copy(g).wait_recv()
+        total = total + long_in[g]
+    out_ref[0:packed, :] = total
+    spot = lax.broadcasted_iota(jnp.int32, (32, 128), 1)
+    extra = jnp.zeros((32, 128), F32)
+    for g in range(3):
+        piece = pltpu.roll(total[32 * g : 32 * g + 32], (128 - 2 * half + 32 * g) % 128, 1)
+        extra = jnp.where((spot >= 32 * g) & (spot < 32 * g + 32), piece, extra)
+    out_ref[packed:cols, :] = extra
 
     def drain(q, _):
         to_partner(q, 0).wait_send()
@@ -372,13 +471,16 @@
         far_mine(q).wait_send()
         direct_copy(q).wait_send()
         mid_copy(q).wait_send()
+
+        @pl.when(lax.rem(q, SIDE) < SIDE - 1)
+        def _():
+            near_copy(q, 0, 1).wait_send()
+
         return 0
 
     lax.fori_loop(0, 2 * (last + 1), drain, 0)
-    for step in range(last + 1):
-        plus_copy(step).wait_send()
-        if step < last:
-            minus_copy(step).wait_send()
+    for g in range(SIDE - 1):
+        long_copy(g).wait_send()
 
 
 def shards(eigvec, links, momentum, weights, spins, peram):
@@ -392,7 +494,7 @@
     zcoord = lax.axis_index(GZ).astype(jnp.int32).reshape(1)
 
     def block_of(q):
-        return pl.BlockSpec((1, 1, 2, n, n), lambda i, sp, mo: (sp[q, 0], sp[q, 1], 0, 0, 0))
+        return pl.BlockSpec((1, 1, 2, n, n), lambda i, sp, mo: (sp[0, q], sp[1, q], 0, 0, 0))
 
     mix, left, phase = pl.pallas_call(
         functools.partial(prep_kernel, half, scale, (LX, LY, depth)),
@@ -411,13 +513,14 @@
             jax.ShapeDtypeStruct((2, 2, 256, 2 * n), BF16),
             jax.ShapeDtypeStruct((2, 8, plane), F32),
         ],
-    )(spins, momentum, peram, peram, peram, zcoord)
+    )(spins.T, momentum, peram, peram, peram, zcoord)
 
     fields = eigvec.reshape(half, 6, plane).transpose(1, 0, 2)
-    link_rows = links.reshape(54, plane)
+    link_rows = links.reshape(54, 1, plane)
     vm = pl.BlockSpec(memory_space=pltpu.VMEM)
     dma = pltpu.SemaphoreType.DMA
     nq = nz
+    packed = cols - 32
     out = pl.pallas_call(
         main_kernel,
         out_shape=jax.ShapeDtypeStruct((cols, 128), F32),
@@ -433,20 +536,24 @@
             pltpu.VMEM((2, 6, half, plane), BF16),
             pltpu.VMEM((6, plane // 128, n, 128), F32),
             pltpu.VMEM((6, plane // 128, n, 128), F32),
-            pltpu.VMEM((6 * plane, 256), BF16),
-            pltpu.VMEM((cols, 6 * plane), BF16),
-            pltpu.VMEM((nq, 4, cols, 128), BF16),
-            pltpu.VMEM((nq, 2, cols, 128), BF16),
-            pltpu.VMEM((nq, 2, cols, 128), BF16),
-            pltpu.VMEM((nq, cols, 128), BF16),
-            pltpu.VMEM((nq, cols, 128), BF16),
-            pltpu.VMEM((nq, 2, cols, 128), BF16),
-            pltpu.VMEM((2, 8, cols, 128), F32),
-            pltpu.VMEM((8, cols, 128), F32),
-            pltpu.VMEM((8, cols, 128), F32),
+            pltpu.VMEM((4, 768, 256), BF16),
+            pltpu.VMEM((4, 4 * cols, 768), BF16),
+            pltpu.VMEM((4, 4 * cols, 768), BF16),
+            pltpu.VMEM((4 * cols, 256), F32),
+            pltpu.VMEM((nq, 4, packed, 128), BF16),
+            pltpu.VMEM((nq, 2, packed, 128), BF16),
+            pltpu.VMEM((nq, 2, packed, 128), BF16),
+            pltpu.VMEM((nq, packed, 128), BF16),
+            pltpu.VMEM((nq, packed, 128), BF16),
+            pltpu.VMEM((nq, 2, packed, 128), BF16),
+            pltpu.VMEM((nq, packed, 128), BF16),
+            pltpu.VMEM((SIDE, SIDE, packed, 128), BF16),
+            pltpu.VMEM((SIDE, packed, 128), F32),
+            pltpu.VMEM((SIDE, packed, 128), F32),
+            pltpu.VMEM((SIDE, packed, 128), F32),
             dma((2,)), dma((2,)), dma((2,)), dma((2,)),
             dma((nq, 2)), dma((nq, 2)), dma((nq,)), dma((nq,)),
-            dma((nq, 2)), dma((nq, 2)), dma((8,)), dma((8,)), dma((8,)), dma((8,)),
+            dma((nq, 2)), dma((nq, 2)), dma((nq,)), dma((SIDE, SIDE)), dma((SIDE,)), dma((SIDE,)),
         ],
         compiler_params=pltpu.CompilerParams(
             collective_id=0, has_side_effects=True, vmem_limit_bytes=60 * 1024 * 1024

time: 106 us -> 96.7 us (0.912)
  Pallas kernels: 99.2 us -> 92.3 us
  local copies, waits for them, and re-layouts: 5.39 us -> 3.32 us
  other arithmetic: 1.22 us -> 0 us
    pallas_call x1, Pallas kernels: 96.3 us -> 89.5 us  [shards(): pl.pallas_call(main_kernel, out_shape=jax.ShapeDtypeStruct((cols, 128), F...]
    unnamed x2 -> x1, local copies, waits for them, and re-layouts: 3.04 us -> 1.7 us
    unnamed x1 -> x0, other arithmetic: 1.22 us -> none
where the time goes in v1:
time: 96.7 us; the launch traced here: 95.7 us
  Pallas kernels  92.3 us (95%)
  local copies, waits for them, and re-layouts  3.32 us (3%)
    pallas_call x1, Pallas kernels, shards(): pl.pallas_call(main_kernel, out_shape=jax.ShapeDtypeStruct((cols, 128), F...  89.5 us
    pallas_call x1, Pallas kernels, shards(): pl.pallas_call(functools.partial(prep_kernel, half, scale, (LX, LY, depth...  2.88 us

profile of v1, /device:TPU:40, one launch (start us, length us, event | category | flops | bytes accessed | tf_op | source)
XLA Modules:
  0.0 95.7 jit_solution(11776889703792737607)
XLA Ops:
  0.0 1.7 %copy.9 = bf16[48,3,2,1,512]{4,0,2,1,3:T(8,128)(2,1)} copy(bf16[48,3,2,1,512]{4,2,3,1,0:T(2,128)(2,1)} %param.6) | data formatting | bytes 589824 | tf_op args[0]
  1.7 2.9 %shard_map.64 = (bf16[2,2,192,192]{3,2,1,0:T(8,128)(2,1)}, bf16[2,2,256,192]{3,2,1,0:T(8,128)(2,1)}, f32[2,8,512]{2,1,0:T(8,128)}) custom-call(s32[2,3]{1,0:T(2,128)} %bitcast.13, s32[3]{0:T(128)} %moms.1, f32[4,4,2,96,96]{4,3,2,1,0:T(8,128)} %p2.1, f32[4,4,2,96,96]{4,3,2,1,0:T(8,128)} %p2.1, f32[4,4,2,96,96]{4,3,2,1,0:T(8,128)} %p2.1, s32[1]{0:T(128)} %bitcast.4.zc), custom_call_target="tpu_custom_call" | custom-call | tf_op jit(solution)/shard_map/pallas_call | solution.py:499
  4.6 89.5 %shard_map.65 = f32[144,128]{1,0:T(8,128)} custom-call(s32[3]{0:T(128)} %weights.1, bf16[6,48,512]{2,1,0:T(8,128)(2,1)} %bitcast.10, f32[54,1,512]{2,1,0:T(1,128)} %bitcast.12, f32[2,8,512]{2,1,0:T(8,128)} %get-tuple-element.8.phase, bf16[2,2,192,192]{3,2,1,0:T(8,128)(2,1)} %get-tuple-element.9.mix, bf16[2,2,256,192]{3,2,1,0:T(8,128)(2,1)} %get-tuple-element.10.left), custom_call_target="tpu_custom_call" | custom-call | tf_op jit(solution)/shard_map/pallas_call | solution.py:524
  94.0 1.6 %copy.10 = f32[144,96]{0,1:T(8,128)} copy(f32[144,96]{1,0:T(8,128)} %bitcast.11) | data formatting | bytes 110592 | tf_op jit(solution)/shard_map/slice | solution.py:562

commit v2 on v1

--- a/solution.py
+++ b/solution.py
@@ -13,7 +13,7 @@
 LY = 16
 NX = 4
 NZ = 16
-SIDE = 4
+SIDE = 2
 GZ = ("gz_0", "gz_1")
 GROUPS_GZ = ("groups", "gz_0", "gz_1")
 MESH = pl.DeviceIdType.MESH
@@ -21,23 +21,23 @@
 BF16 = jnp.bfloat16
 
 
-def prep_kernel(half, scale, sizes, spins, moms, p0, p1, p2, zc, mix_ref, left_ref, phase_ref):
-    del spins
-    ea = lax.axis_index("ea")
-
+def prepare(half, scale, sizes, ea, along_z, spins, moms, pbuf, mix_ref, left_ref, phase_ref):
     def split(ref, at, value):
         high = value.astype(BF16)
         ref[0, at, :] = high
         ref[1, at, :] = (value - high.astype(F32)).astype(BF16)
 
-    n = p0.shape[-1]
-    for slot, p in ((0, p1), (1, p2)):
-        re = p[0, 0, 0].T
-        im = p[0, 0, 1].T
+    n = pbuf.shape[-1]
+
+    def block(q, part):
+        return pbuf[spins[0, q], spins[1, q], part].T
+
+    for slot, q in ((0, 1), (1, 2)):
+        re, im = block(q, 0), block(q, 1)
         split(mix_ref.at[slot], slice(0, n), jnp.concatenate([re, -im], 1))
         split(mix_ref.at[slot], slice(n, 2 * n), jnp.concatenate([im, re], 1))
-    re = p0[0, 0, 0].T * scale
-    im = p0[0, 0, 1].T * scale
+    re = block(0, 0) * scale
+    im = block(0, 1) * scale
     first = ea == 0
     pad = jnp.zeros((128 - 2 * half, 2 * n), F32)
     for own in range(2):
@@ -51,11 +51,11 @@
         split(left_ref.at[1], slice(own * 128, own * 128 + 128), jnp.concatenate([-imag, real, pad], 0))
     lx, ly, depth = sizes
     sites = lax.broadcasted_iota(jnp.int32, (8, lx * ly), 1)
-    xcoord = sites % lx
-    ycoord = sites // lx
+    xcoord = lax.rem(sites, lx)
+    ycoord = lax.div(sites, lx)
     two_pi = 2.0 * math.pi
     inplane = (moms[0] * xcoord).astype(F32) / lx + (moms[1] * ycoord).astype(F32) / ly
-    along = jnp.full((8, lx * ly), moms[2] * zc[0], jnp.int32).astype(F32)
+    along = jnp.full((8, lx * ly), moms[2] * along_z, jnp.int32).astype(F32)
     angle = two_pi * inplane + two_pi * along / depth
     phase_ref[0] = jnp.cos(angle)
     phase_ref[1] = jnp.sin(angle)
@@ -70,10 +70,11 @@
 
 
 def main_kernel(
-    weights, v_ref, links, phase, mix, left, out_ref,
+    scale, weights, spins, moms, v_ref, links, peram, out_ref,
+    pbuf, phase, mix, left,
     vall, upper, lower, back, disp, phown, phall, v1, v2, lmat, wbuf0, wbuf1, acc,
-    grid_in, mine, grid_out, far_in, mid_out, x_in, near_out, near_in, near_own, long_out, long_in,
-    halo_s, halo_r, ea_s, ea_r, dd_s, dd_r, fx_s, fx_r, x_s, x_r, near_s, near_r, long_s, long_r,
+    grid_in, mine, grid_out, far_in, mid_out, x_in, near_out, near_in, near_own, ring_out, plus_in, minus_in,
+    p_sem, halo_s, halo_r, ea_s, ea_r, dd_s, dd_r, fx_s, fx_r, x_s, x_r, near_s, near_r, plus_s, plus_r, minus_s, minus_r,
 ):
     ncomp, half, plane = v_ref.shape
     cols = out_ref.shape[0]
@@ -99,14 +100,11 @@
     site_up = {"gz_0": gup // nz, "gz_1": lax.rem(gup, nz)}
     site_dn = {"gz_0": gdn // nz, "gz_1": lax.rem(gdn, nz)}
 
-    def in_side(r):
-        return {"gz_1": zh * SIDE + lax.rem(zl + r, SIDE)}
-
-    def across(r):
-        return {"gz_1": lax.rem(zh + r, SIDE) * SIDE + zl}
-
-    def turn_of(n):
-        return jnp.where(n == 0, 2, jnp.where(n == 1, 1, jnp.where(n == 2, 3, 0)))
+    nh = nz // SIDE
+    pair = {"gz_1": zh * SIDE + 1 - zl}
+    ring_up = {"gz_1": lax.rem(zh + 1, nh) * SIDE + zl}
+    ring_dn = {"gz_1": lax.rem(zh + nh - 1, nh) * SIDE + zl}
+    ring = 4
 
     def remote(src, dst, s, r, to):
         return pltpu.make_async_remote_copy(
@@ -115,19 +113,38 @@
 
     barrier = pltpu.get_barrier_semaphore()
     peers = [partner, to_xp, to_xm, site_up, site_dn]
-    for r in range(1, SIDE):
-        peers.append(in_side(r))
-        peers.append(across(r))
+    peers += [pair, ring_up, ring_dn]
     for to in peers:
         pl.semaphore_signal(barrier, inc=1, device_id=to, device_id_type=MESH)
     pl.semaphore_wait(barrier, len(peers))
 
-    send_v = remote(v_ref, upper, halo_s.at[0], halo_r.at[0], site_dn)
-    send_v.start()
+    rows = 16
+    chunks = half // rows
+
+    def chunk_of(ref, t):
+        return ref.at[:, pl.ds(t * rows, rows), :]
+
+    def v_copy(t):
+        return remote(
+            chunk_of(v_ref, t), chunk_of(upper, t), halo_s.at[0, t], halo_r.at[0, t], site_dn
+        )
+
+    def b_copy(t):
+        return remote(
+            chunk_of(back, t), chunk_of(lower, t), halo_s.at[1, t], halo_r.at[1, t], site_up
+        )
+
+    def ph_copy(t):
+        return remote(
+            chunk_of(phown, t), chunk_of(phall.at[e], t), ea_s.at[1 + t], ea_r.at[1 + t], partner
+        )
+
+    for t in range(chunks):
+        v_copy(t).start()
+    fetch = pltpu.make_async_copy(peram, pbuf, p_sem)
+    fetch.start()
     send_ea = remote(v_ref, vall.at[e], ea_s.at[0], ea_r.at[0], partner)
     send_ea.start()
-
-    rows = 16
 
     def field(ref, r0):
         return [ref[c, pl.ds(r0, rows), :].astype(F32) for c in range(ncomp)]
@@ -157,18 +174,19 @@
             out += [re, im]
         return out
 
-    def back_tile(t, _):
-        r0 = pl.multiple_of(t * rows, rows)
+    def back_tile(t):
+        r0 = t * rows
         f = field(v_ref, r0)
         for c, val in enumerate(adjoint(2, f)):
             back[c, pl.ds(r0, rows), :] = val.astype(BF16)
         for c in range(ncomp):
             vall[e, c, pl.ds(r0, rows), :] = v_ref[c, pl.ds(r0, rows), :]
-        return 0
-
-    lax.fori_loop(0, half // rows, back_tile, 0)
-    send_b = remote(back, lower, halo_s.at[1], halo_r.at[1], site_up)
-    send_b.start()
+
+    for t in range(chunks):
+        back_tile(t)
+        b_copy(t).start()
+    fetch.wait()
+    prepare(half, scale, (LX, LY, nx * nz), e, gz, spins, moms, pbuf, mix, left, phase)
 
     lane = lax.broadcasted_iota(jnp.int32, (rows, plane), 1)
     xc = lax.rem(lane, LX)
@@ -212,8 +230,10 @@
                     dst[2 * k + r, lt] = part[:, lt * 128 : lt * 128 + 128]
 
     def dest_z(q):
-        hop = lax.rem(zh + turn_of(q // SIDE), SIDE)
-        return hop * SIDE + lax.rem(zl + turn_of(lax.rem(q, SIDE)), SIDE)
+        step = q // 2
+        hop = step // 2
+        to = jnp.where(lax.rem(step, 2) == 0, zh + ring - hop, zh + 1 - ring + hop + nh)
+        return lax.rem(to, nh) * SIDE + jnp.where(lax.rem(q, 2) == 0, 1 - zl, zl)
 
     turns = 4
 
@@ -333,55 +353,50 @@
 
     last = 7
 
-    def near_copy(q, g, r):
-        return remote(near_out.at[q], near_in.at[g, r], near_s.at[q], near_r.at[g, r], in_side(r))
+    def near_copy(step):
+        return remote(near_out.at[step], near_in.at[step], near_s.at[step], near_r.at[step], pair)
 
     def near_sum(step):
-        for par in range(2):
-            q = 2 * step + par
-            g = q // SIDE
-            r = turn_of(lax.rem(q, SIDE))
-            total = x_sum(q)
-            if par == 0:
-                near_out[q] = total.astype(BF16)
-                near_copy(q, g, r).start()
-            else:
-
-                @pl.when(r > 0)
-                def _():
-                    near_out[q] = total.astype(BF16)
-                    near_copy(q, g, r).start()
-
-                @pl.when(r == 0)
-                def _():
-                    near_own[g] = total
-
-    def long_copy(g):
+        near_out[step] = x_sum(2 * step).astype(BF16)
+        near_copy(step).start()
+        near_own[step] = x_sum(2 * step + 1)
+
+    def plus_copy(hop):
         return remote(
-            long_out.at[g], long_in.at[g], long_s.at[g], long_r.at[g], across(turn_of(g))
-        )
-
-    def long_sum(g):
-        total = near_own[g]
-        for r in range(1, SIDE):
-            near_copy(0, g, r).wait_recv()
-            total = total + near_in[g, r].astype(F32)
-        near_own[g] = total
-
-        @pl.when(g < SIDE - 1)
-        def _():
-            long_out[g] = near_own[g]
-            long_copy(g).start()
+            ring_out.at[0, hop], plus_in.at[hop], plus_s.at[hop], plus_r.at[hop], ring_up
+        )
+
+    def minus_copy(hop):
+        return remote(
+            ring_out.at[1, hop], minus_in.at[hop], minus_s.at[hop], minus_r.at[hop], ring_dn
+        )
+
+    def ring_step(side, hop):
+        step = 2 * hop + side
+        copy, arrived = ((plus_copy, plus_in), (minus_copy, minus_in))[side]
+        near_copy(step).wait_recv()
+        ring_out[side, hop] = near_own[step] + near_in[step].astype(F32)
+
+        @pl.when(hop > 0)
+        def _():
+            copy(hop - 1).wait_recv()
+            ring_out[side, hop] += arrived[hop - 1]
+
+        if side == 0:
+            copy(hop).start()
+        else:
+
+            @pl.when(hop < ring - 1)
+            def _():
+                copy(hop).start()
 
     w_only(wbuf0, 0)
     lax.fori_loop(0, half // rows, inplane_tile, 0)
-    send_v.wait()
-    send_b.wait()
     cosine = phase[0, 0:1]
     sine = phase[1, 0:1]
 
-    def zdir_tile(t, _):
-        r0 = pl.multiple_of(t * rows, rows)
+    def zdir_tile(t):
+        r0 = t * rows
         ahead = apply(2, field(upper, r0))
         low = field(lower, r0)
         tot = [
@@ -394,12 +409,14 @@
             phown[2 * k + 1, pl.ds(r0, rows), :] = (cosine * im - sine * re).astype(BF16)
         for c in range(ncomp):
             phall[e, c, pl.ds(r0, rows), :] = phown[c, pl.ds(r0, rows), :]
-        return 0
-
-    lax.fori_loop(0, half // rows, zdir_tile, 0)
-    send_ph = remote(phown, phall.at[e], ea_s.at[1], ea_r.at[1], partner)
-    send_ph.start()
-    send_ph.wait()
+
+    for t in range(chunks):
+        v_copy(t).wait_recv()
+        b_copy(t).wait_recv()
+        zdir_tile(t)
+        ph_copy(t).start()
+    for t in range(chunks):
+        ph_copy(t).wait_recv()
     for k in range(3):
         stack = jnp.concatenate(
             [phall[0, 2 * k], phall[1, 2 * k], phall[0, 2 * k + 1], phall[1, 2 * k + 1]], 0
@@ -444,19 +461,21 @@
     def body(i, _):
         stage(2 * i, wbuf0, wbuf1)
 
+        @pl.when(i >= 4)
+        def _():
+            ring_step(1, i - 4)
+
         stage(2 * i + 1, wbuf1, wbuf0)
 
-        @pl.when(i >= 3)
-        def _():
-            long_sum(i - 3)
+        @pl.when((i >= 3) & (i <= 6))
+        def _():
+            ring_step(0, i - 3)
 
         return 0
 
-    lax.fori_loop(0, 7, body, 0)
-    total = near_own[SIDE - 1]
-    for g in range(SIDE - 1):
-        long_copy(g).wait_recv()
-        total = total + long_in[g]
+    lax.fori_loop(0, 8, body, 0)
+    plus_copy(ring - 1).wait_recv()
+    total = ring_out[1, ring - 1] + plus_in[ring - 1]
     out_ref[0:packed, :] = total
     spot = lax.broadcasted_iota(jnp.int32, (32, 128), 1)
     extra = jnp.zeros((32, 128), F32)
@@ -472,15 +491,19 @@
         direct_copy(q).wait_send()
         mid_copy(q).wait_send()
 
-        @pl.when(lax.rem(q, SIDE) < SIDE - 1)
-        def _():
-            near_copy(q, 0, 1).wait_send()
-
         return 0
 
     lax.fori_loop(0, 2 * (last + 1), drain, 0)
-    for g in range(SIDE - 1):
-        long_copy(g).wait_send()
+    for t in range(chunks):
+        v_copy(t).wait_send()
+        b_copy(t).wait_send()
+        ph_copy(t).wait_send()
+    for step in range(last + 1):
+        near_copy(step).wait_send()
+    for hop in range(ring):
+        plus_copy(hop).wait_send()
+        if hop < ring - 1:
+            minus_copy(hop).wait_send()
 
 
 def shards(eigvec, links, momentum, weights, spins, peram):
@@ -491,30 +514,6 @@
     depth = nx * nz
     cols = n * n // depth
     scale = 1.0 / math.sqrt(LX * LY * depth)
-    zcoord = lax.axis_index(GZ).astype(jnp.int32).reshape(1)
-
-    def block_of(q):
-        return pl.BlockSpec((1, 1, 2, n, n), lambda i, sp, mo: (sp[0, q], sp[1, q], 0, 0, 0))
-
-    mix, left, phase = pl.pallas_call(
-        functools.partial(prep_kernel, half, scale, (LX, LY, depth)),
-        grid_spec=pltpu.PrefetchScalarGridSpec(
-            num_scalar_prefetch=2,
-            grid=(1,),
-            in_specs=[block_of(0), block_of(1), block_of(2), pl.BlockSpec(memory_space=pltpu.SMEM)],
-            out_specs=[
-                pl.BlockSpec((2, 2, 2 * n, 2 * n), lambda i, sp, mo: (0, 0, 0, 0)),
-                pl.BlockSpec((2, 2, 256, 2 * n), lambda i, sp, mo: (0, 0, 0, 0)),
-                pl.BlockSpec((2, 8, plane), lambda i, sp, mo: (0, 0, 0)),
-            ],
-        ),
-        out_shape=[
-            jax.ShapeDtypeStruct((2, 2, 2 * n, 2 * n), BF16),
-            jax.ShapeDtypeStruct((2, 2, 256, 2 * n), BF16),
-            jax.ShapeDtypeStruct((2, 8, plane), F32),
-        ],
-    )(spins.T, momentum, peram, peram, peram, zcoord)
-
     fields = eigvec.reshape(half, 6, plane).transpose(1, 0, 2)
     link_rows = links.reshape(54, 1, plane)
     vm = pl.BlockSpec(memory_space=pltpu.VMEM)
@@ -522,11 +521,15 @@
     nq = nz
     packed = cols - 32
     out = pl.pallas_call(
-        main_kernel,
+        functools.partial(main_kernel, scale),
         out_shape=jax.ShapeDtypeStruct((cols, 128), F32),
-        in_specs=[pl.BlockSpec(memory_space=pltpu.SMEM)] + [vm] * 5,
+        in_specs=[pl.BlockSpec(memory_space=pltpu.SMEM)] * 3 + [vm] * 2 + [pl.BlockSpec(memory_space=pl.ANY)],
         out_specs=vm,
         scratch_shapes=[
+            pltpu.VMEM(peram.shape, F32),
+            pltpu.VMEM((2, 8, plane), F32),
+            pltpu.VMEM((2, 2, 2 * n, 2 * n), BF16),
+            pltpu.VMEM((2, 2, 256, 2 * n), BF16),
             pltpu.VMEM((2, 6, half, plane), BF16),
             pltpu.VMEM((6, half, plane), BF16),
             pltpu.VMEM((6, half, plane), BF16),
@@ -546,19 +549,20 @@
             pltpu.VMEM((nq, packed, 128), BF16),
             pltpu.VMEM((nq, packed, 128), BF16),
             pltpu.VMEM((nq, 2, packed, 128), BF16),
-            pltpu.VMEM((nq, packed, 128), BF16),
-            pltpu.VMEM((SIDE, SIDE, packed, 128), BF16),
-            pltpu.VMEM((SIDE, packed, 128), F32),
-            pltpu.VMEM((SIDE, packed, 128), F32),
-            pltpu.VMEM((SIDE, packed, 128), F32),
-            dma((2,)), dma((2,)), dma((2,)), dma((2,)),
+            pltpu.VMEM((8, packed, 128), BF16),
+            pltpu.VMEM((8, packed, 128), BF16),
+            pltpu.VMEM((8, packed, 128), F32),
+            pltpu.VMEM((2, 4, packed, 128), F32),
+            pltpu.VMEM((4, packed, 128), F32),
+            pltpu.VMEM((4, packed, 128), F32),
+            dma, dma((2, 3)), dma((2, 3)), dma((4,)), dma((4,)),
             dma((nq, 2)), dma((nq, 2)), dma((nq,)), dma((nq,)),
-            dma((nq, 2)), dma((nq, 2)), dma((nq,)), dma((SIDE, SIDE)), dma((SIDE,)), dma((SIDE,)),
+            dma((nq, 2)), dma((nq, 2)), dma((8,)), dma((8,)), dma((4,)), dma((4,)), dma((4,)), dma((4,)),
         ],
         compiler_params=pltpu.CompilerParams(
             collective_id=0, has_side_effects=True, vmem_limit_bytes=60 * 1024 * 1024
         ),
-    )(weights, fields, link_rows, phase, mix, left)
+    )(weights, spins.T, momentum, fields, link_rows, peram)
     return out[:, :n].reshape(cols, 2, half).transpose(1, 2, 0)
 
 

time: 96.7 us -> 84.6 us (0.87)
  Pallas kernels: 92.3 us -> 81.1 us
    pallas_call x2 -> x1, Pallas kernels: 92.3 us -> 81.1 us  [shards(): pl.pallas_call(functools.partial(main_kernel, scale), out_shape=jax.Shape...]
where the time goes in v2:
time: 84.6 us; the launch traced here: 84.4 us
  Pallas kernels  81.1 us (96%)
  local copies, waits for them, and re-layouts  3.32 us (4%)
    pallas_call x1, Pallas kernels, shards(): pl.pallas_call(functools.partial(main_kernel, scale), out_shape=jax.Shape...  81.1 us
    unnamed x1, local copies, waits for them, and re-layouts  1.7 us

profile of v2, /device:TPU:40, one launch (start us, length us, event | category | flops | bytes accessed | tf_op | source)
XLA Modules:
  0.0 84.4 jit_solution(6791205811786872669)
XLA Ops:
  0.0 1.7 %copy.9 = bf16[48,3,2,1,512]{4,0,2,1,3:T(8,128)(2,1)} copy(bf16[48,3,2,1,512]{4,2,3,1,0:T(2,128)(2,1)} %param.6) | data formatting | bytes 589824 | tf_op args[0]
  1.7 81.1 %shard_map.64 = f32[144,128]{1,0:T(8,128)} custom-call(s32[3]{0:T(128)} %weights.1, s32[2,3]{1,0:T(2,128)} %bitcast.12, s32[3]{0:T(128)} %moms.1, bf16[6,48,512]{2,1,0:T(8,128)(2,1)} %bitcast.9, f32[54,1,512]{2,1,0:T(1,128)} %bitcast.11, f32[4,4,2,96,96]{4,3,2,1,0:T(8,128)} %peram.1), custom_call_target="tpu_custom_call" | custom-call | tf_op jit(solution)/shard_map/pallas_call | solution.py:523
  82.8 1.6 %copy.10 = f32[144,96]{0,1:T(8,128)} copy(f32[144,96]{1,0:T(8,128)} %bitcast.10) | data formatting | bytes 110592 | tf_op jit(solution)/shard_map/slice | solution.py:566

commit v3 on v2

--- a/solution.py
+++ b/solution.py
@@ -73,7 +73,7 @@
     scale, weights, spins, moms, v_ref, links, peram, out_ref,
     pbuf, phase, mix, left,
     vall, upper, lower, back, disp, phown, phall, v1, v2, lmat, wbuf0, wbuf1, acc,
-    grid_in, mine, grid_out, far_in, mid_out, x_in, near_out, near_in, near_own, ring_out, plus_in, minus_in,
+    grid_in, mine, grid_out, far_in, mid_out, x_in, near_out, near_in, near_own, ring_out, plus_in, minus_in, short_out, plus_short, minus_short,
     p_sem, halo_s, halo_r, ea_s, ea_r, dd_s, dd_r, fx_s, fx_r, x_s, x_r, near_s, near_r, plus_s, plus_r, minus_s, minus_r,
 ):
     ncomp, half, plane = v_ref.shape
@@ -269,15 +269,16 @@
     def dot_turn(src, k):
         acc[...] += jnp.dot(src[k], lmat[k], preferred_element_type=F32)
 
-    def fused(src, dst, step):
-        acc[...] = jnp.zeros_like(acc)
+    def fused(src, dst, step, part):
+        if part == 0:
+            acc[...] = jnp.zeros_like(acc)
 
         def turn(k, _):
             dot_turn(src, k)
             w_section(dst, step + 1, k)
             return 0
 
-        lax.fori_loop(0, turns, turn, 0)
+        lax.fori_loop(part * 2, part * 2 + 2, turn, 0)
 
     def dot_only(src):
         acc[...] = jnp.zeros_like(acc)
@@ -361,34 +362,46 @@
         near_copy(step).start()
         near_own[step] = x_sum(2 * step + 1)
 
-    def plus_copy(hop):
+    early = 2
+    ring_s, ring_r = (plus_s, minus_s), (plus_r, minus_r)
+    ring_to = (ring_up, ring_dn)
+    short_in, full_in = (plus_short, minus_short), (plus_in, minus_in)
+
+    def short_copy(side, hop):
         return remote(
-            ring_out.at[0, hop], plus_in.at[hop], plus_s.at[hop], plus_r.at[hop], ring_up
-        )
-
-    def minus_copy(hop):
+            short_out.at[side, hop], short_in[side].at[hop],
+            ring_s[side].at[hop], ring_r[side].at[hop], ring_to[side],
+        )
+
+    def full_copy(side, hop):
         return remote(
-            ring_out.at[1, hop], minus_in.at[hop], minus_s.at[hop], minus_r.at[hop], ring_dn
+            ring_out.at[side, hop], full_in[side].at[hop],
+            ring_s[side].at[hop], ring_r[side].at[hop], ring_to[side],
         )
 
     def ring_step(side, hop):
         step = 2 * hop + side
-        copy, arrived = ((plus_copy, plus_in), (minus_copy, minus_in))[side]
         near_copy(step).wait_recv()
         ring_out[side, hop] = near_own[step] + near_in[step].astype(F32)
 
-        @pl.when(hop > 0)
-        def _():
-            copy(hop - 1).wait_recv()
-            ring_out[side, hop] += arrived[hop - 1]
-
-        if side == 0:
-            copy(hop).start()
-        else:
-
-            @pl.when(hop < ring - 1)
-            def _():
-                copy(hop).start()
+        @pl.when((hop > 0) & (hop <= early))
+        def _():
+            short_copy(side, hop - 1).wait_recv()
+            ring_out[side, hop] += short_in[side][hop - 1].astype(F32)
+
+        @pl.when(hop > early)
+        def _():
+            full_copy(side, hop - 1).wait_recv()
+            ring_out[side, hop] += full_in[side][hop - 1]
+
+        @pl.when(hop < early)
+        def _():
+            short_out[side, hop] = ring_out[side, hop].astype(BF16)
+            short_copy(side, hop).start()
+
+        @pl.when((hop >= early) & (hop < ring - side))
+        def _():
+            full_copy(side, hop).start()
 
     w_only(wbuf0, 0)
     lax.fori_loop(0, half // rows, inplane_tile, 0)
@@ -434,47 +447,51 @@
     def stage(step, src, dst):
         @pl.when(step < last)
         def _():
-            fused(src, dst, step)
-
-        @pl.when(step == last)
-        def _():
-            dot_only(src)
+            fused(src, dst, step, 0)
 
         @pl.when((step >= 1) & (step <= last + 1))
         def _():
             first_x(2 * (step - 1))
             first_x(2 * (step - 1) + 1)
 
+        @pl.when((step >= 4) & (step <= last + 4))
+        def _():
+            near_sum(step - 4)
+
+        @pl.when(step < last)
+        def _():
+            fused(src, dst, step, 1)
+
+        @pl.when(step == last)
+        def _():
+            dot_only(src)
+
         @pl.when(step <= last)
         def _():
             give(step)
 
-        @pl.when((step >= 3) & (step <= last + 3))
-        def _():
-            second_x(2 * (step - 3))
-            second_x(2 * (step - 3) + 1)
-
-        @pl.when((step >= 5) & (step <= last + 5))
-        def _():
-            near_sum(step - 5)
+        @pl.when((step >= 2) & (step <= last + 2))
+        def _():
+            second_x(2 * (step - 2))
+            second_x(2 * (step - 2) + 1)
 
     def body(i, _):
         stage(2 * i, wbuf0, wbuf1)
 
-        @pl.when(i >= 4)
-        def _():
-            ring_step(1, i - 4)
+        @pl.when(i >= 3)
+        def _():
+            ring_step(1, i - 3)
 
         stage(2 * i + 1, wbuf1, wbuf0)
 
-        @pl.when((i >= 3) & (i <= 6))
-        def _():
-            ring_step(0, i - 3)
+        @pl.when((i >= 2) & (i <= 5))
+        def _():
+            ring_step(0, i - 2)
 
         return 0
 
-    lax.fori_loop(0, 8, body, 0)
-    plus_copy(ring - 1).wait_recv()
+    lax.fori_loop(0, 7, body, 0)
+    full_copy(0, ring - 1).wait_recv()
     total = ring_out[1, ring - 1] + plus_in[ring - 1]
     out_ref[0:packed, :] = total
     spot = lax.broadcasted_iota(jnp.int32, (32, 128), 1)
@@ -500,10 +517,9 @@
         ph_copy(t).wait_send()
     for step in range(last + 1):
         near_copy(step).wait_send()
-    for hop in range(ring):
-        plus_copy(hop).wait_send()
-        if hop < ring - 1:
-            minus_copy(hop).wait_send()
+    for side in range(2):
+        for hop in range(ring - side):
+            (short_copy if hop < early else full_copy)(side, hop).wait_send()
 
 
 def shards(eigvec, links, momentum, weights, spins, peram):
@@ -555,6 +571,9 @@
             pltpu.VMEM((2, 4, packed, 128), F32),
             pltpu.VMEM((4, packed, 128), F32),
             pltpu.VMEM((4, packed, 128), F32),
+            pltpu.VMEM((2, 2, packed, 128), BF16),
+            pltpu.VMEM((2, packed, 128), BF16),
+            pltpu.VMEM((2, packed, 128), BF16),
             dma, dma((2, 3)), dma((2, 3)), dma((4,)), dma((4,)),
             dma((nq, 2)), dma((nq, 2)), dma((nq,)), dma((nq,)),
             dma((nq, 2)), dma((nq, 2)), dma((8,)), dma((8,)), dma((4,)), dma((4,)), dma((4,)), dma((4,)),

time: 84.6 us -> 83.7 us (0.989)
  Pallas kernels: 81.1 us -> 80.1 us
    pallas_call x1, Pallas kernels: 81.1 us -> 80.1 us  [shards(): pl.pallas_call(functools.partial(main_kernel, scale), out_shape=jax.Shape...]
where the time goes in v3:
time: 83.7 us; the launch traced here: 83.5 us
  Pallas kernels  80.1 us (96%)
  local copies, waits for them, and re-layouts  3.32 us (4%)
    pallas_call x1, Pallas kernels, shards(): pl.pallas_call(functools.partial(main_kernel, scale), out_shape=jax.Shape...  80.1 us
    unnamed x1, local copies, waits for them, and re-layouts  1.7 us

profile of v3, /device:TPU:40, one launch (start us, length us, event | category | flops | bytes accessed | tf_op | source)
XLA Modules:
  0.0 83.5 jit_solution(11894171533555321705)
XLA Ops:
  0.0 1.7 %copy.9 = bf16[48,3,2,1,512]{4,0,2,1,3:T(8,128)(2,1)} copy(bf16[48,3,2,1,512]{4,2,3,1,0:T(2,128)(2,1)} %param.6) | data formatting | bytes 589824 | tf_op args[0]
  1.7 80.1 %shard_map.64 = f32[144,128]{1,0:T(8,128)} custom-call(s32[3]{0:T(128)} %weights.1, s32[2,3]{1,0:T(2,128)} %bitcast.12, s32[3]{0:T(128)} %moms.1, bf16[6,48,512]{2,1,0:T(8,128)(2,1)} %bitcast.9, f32[54,1,512]{2,1,0:T(1,128)} %bitcast.11, f32[4,4,2,96,96]{4,3,2,1,0:T(8,128)} %peram.1), custom_call_target="tpu_custom_call" | custom-call | tf_op jit(solution)/shard_map/pallas_call | solution.py:539
  81.8 1.6 %copy.10 = f32[144,96]{0,1:T(8,128)} copy(f32[144,96]{1,0:T(8,128)} %bitcast.10) | data formatting | bytes 110592 | tf_op jit(solution)/shard_map/slice | solution.py:585

commit v4 on v3

--- a/solution.py
+++ b/solution.py
@@ -229,10 +229,16 @@
                 for lt in range(plane // 128):
                     dst[2 * k + r, lt] = part[:, lt * 128 : lt * 128 + 128]
 
+    def is_minus(step):
+        return (step == 3) | (step >= 5)
+
+    def hop_of(step):
+        return jnp.where(step < 3, step, jnp.where(step == 3, 0, jnp.where(step == 4, 3, step - 4)))
+
     def dest_z(q):
         step = q // 2
-        hop = step // 2
-        to = jnp.where(lax.rem(step, 2) == 0, zh + ring - hop, zh + 1 - ring + hop + nh)
+        hop = hop_of(step)
+        to = jnp.where(is_minus(step), zh + 1 - ring + hop + nh, zh + ring - hop)
         return lax.rem(to, nh) * SIDE + jnp.where(lax.rem(q, 2) == 0, 1 - zl, zl)
 
     turns = 4
@@ -379,8 +385,7 @@
             ring_s[side].at[hop], ring_r[side].at[hop], ring_to[side],
         )
 
-    def ring_step(side, hop):
-        step = 2 * hop + side
+    def ring_step(side, hop, step):
         near_copy(step).wait_recv()
         ring_out[side, hop] = near_own[step] + near_in[step].astype(F32)
 
@@ -475,19 +480,24 @@
             second_x(2 * (step - 2))
             second_x(2 * (step - 2) + 1)
 
+    def ring_at(step):
+        inside = (step >= 0) & (step <= last)
+
+        @pl.when(inside & jnp.logical_not(is_minus(step)))
+        def _():
+            ring_step(0, hop_of(step), step)
+
+        @pl.when(inside & is_minus(step))
+        def _():
+            ring_step(1, hop_of(step), step)
+
     def body(i, _):
         stage(2 * i, wbuf0, wbuf1)
 
-        @pl.when(i >= 3)
-        def _():
-            ring_step(1, i - 3)
-
+        ring_at(2 * i - 5)
         stage(2 * i + 1, wbuf1, wbuf0)
 
-        @pl.when((i >= 2) & (i <= 5))
-        def _():
-            ring_step(0, i - 2)
-
+        ring_at(2 * i - 4)
         return 0
 
     lax.fori_loop(0, 7, body, 0)

time: 83.7 us -> 82.7 us (0.988)
  Pallas kernels: 80.1 us -> 78.8 us
    pallas_call x1, Pallas kernels: 80.1 us -> 78.8 us  [shards(): pl.pallas_call(functools.partial(main_kernel, scale), out_shape=jax.Shape...]
where the time goes in v4:
time: 82.7 us; the launch traced here: 82.1 us
  Pallas kernels  78.8 us (95%)
  local copies, waits for them, and re-layouts  3.32 us (4%)
    pallas_call x1, Pallas kernels, shards(): pl.pallas_call(functools.partial(main_kernel, scale), out_shape=jax.Shape...  78.8 us
    unnamed x1, local copies, waits for them, and re-layouts  1.7 us

profile of v4, /device:TPU:40, one launch (start us, length us, event | category | flops | bytes accessed | tf_op | source)
XLA Modules:
  0.0 82.1 jit_solution(15936020394106462667)
XLA Ops:
  0.0 1.7 %copy.9 = bf16[48,3,2,1,512]{4,0,2,1,3:T(8,128)(2,1)} copy(bf16[48,3,2,1,512]{4,2,3,1,0:T(2,128)(2,1)} %param.6) | data formatting | bytes 589824 | tf_op args[0]
  1.7 78.8 %shard_map.64 = f32[144,128]{1,0:T(8,128)} custom-call(s32[3]{0:T(128)} %weights.1, s32[2,3]{1,0:T(2,128)} %bitcast.12, s32[3]{0:T(128)} %moms.1, bf16[6,48,512]{2,1,0:T(8,128)(2,1)} %bitcast.9, f32[54,1,512]{2,1,0:T(1,128)} %bitcast.11, f32[4,4,2,96,96]{4,3,2,1,0:T(8,128)} %peram.1), custom_call_target="tpu_custom_call" | custom-call | tf_op jit(solution)/shard_map/pallas_call | solution.py:549
  80.5 1.6 %copy.10 = f32[144,96]{0,1:T(8,128)} copy(f32[144,96]{1,0:T(8,128)} %bitcast.10) | data formatting | bytes 110592 | tf_op jit(solution)/shard_map/slice | solution.py:595

commit v5 on v4

--- a/solution.py
+++ b/solution.py
@@ -72,7 +72,7 @@
 def main_kernel(
     scale, weights, spins, moms, v_ref, links, peram, out_ref,
     pbuf, phase, mix, left,
-    vall, upper, lower, back, disp, phown, phall, v1, v2, lmat, wbuf0, wbuf1, acc,
+    vall, upper, lower, back, disp, phown, phall, v1, v2, lmat, wbuf0, wbuf1, wbuf2, acc,
     grid_in, mine, grid_out, far_in, mid_out, x_in, near_out, near_in, near_own, ring_out, plus_in, minus_in, short_out, plus_short, minus_short,
     p_sem, halo_s, halo_r, ea_s, ea_r, dd_s, dd_r, fx_s, fx_r, x_s, x_r, near_s, near_r, plus_s, plus_r, minus_s, minus_r,
 ):
@@ -281,7 +281,7 @@
 
         def turn(k, _):
             dot_turn(src, k)
-            w_section(dst, step + 1, k)
+            w_section(dst, step + 2, k)
             return 0
 
         lax.fori_loop(part * 2, part * 2 + 2, turn, 0)
@@ -410,6 +410,7 @@
 
     w_only(wbuf0, 0)
     lax.fori_loop(0, half // rows, inplane_tile, 0)
+    w_only(wbuf1, 1)
     cosine = phase[0, 0:1]
     sine = phase[1, 0:1]
 
@@ -450,7 +451,7 @@
                 lmat[piece // 3, at : at + 256, :] = turned[hf * 256 : hf * 256 + 256]
 
     def stage(step, src, dst):
-        @pl.when(step < last)
+        @pl.when(step < last - 1)
         def _():
             fused(src, dst, step, 0)
 
@@ -463,11 +464,11 @@
         def _():
             near_sum(step - 4)
 
-        @pl.when(step < last)
+        @pl.when(step < last - 1)
         def _():
             fused(src, dst, step, 1)
 
-        @pl.when(step == last)
+        @pl.when((step >= last - 1) & (step <= last))
         def _():
             dot_only(src)
 
@@ -491,16 +492,15 @@
         def _():
             ring_step(1, hop_of(step), step)
 
+    bufs = (wbuf0, wbuf1, wbuf2)
+
     def body(i, _):
-        stage(2 * i, wbuf0, wbuf1)
-
-        ring_at(2 * i - 5)
-        stage(2 * i + 1, wbuf1, wbuf0)
-
-        ring_at(2 * i - 4)
+        for u in range(3):
+            stage(3 * i + u, bufs[u], bufs[(u + 2) % 3])
+            ring_at(3 * i + u - 5)
         return 0
 
-    lax.fori_loop(0, 7, body, 0)
+    lax.fori_loop(0, 5, body, 0)
     full_copy(0, ring - 1).wait_recv()
     total = ring_out[1, ring - 1] + plus_in[ring - 1]
     out_ref[0:packed, :] = total
@@ -568,6 +568,7 @@
             pltpu.VMEM((4, 768, 256), BF16),
             pltpu.VMEM((4, 4 * cols, 768), BF16),
             pltpu.VMEM((4, 4 * cols, 768), BF16),
+            pltpu.VMEM((4, 4 * cols, 768), BF16),
             pltpu.VMEM((4 * cols, 256), F32),
             pltpu.VMEM((nq, 4, packed, 128), BF16),
             pltpu.VMEM((nq, 2, packed, 128), BF16),

time: 82.7 us -> 83.5 us (level)
  no operation moved by 1% of the time
where the time goes in v5:
time: 83.5 us; the launch traced here: 82.9 us
  Pallas kernels  79.5 us (95%)
  local copies, waits for them, and re-layouts  3.32 us (4%)
    pallas_call x1, Pallas kernels, shards(): pl.pallas_call(functools.partial(main_kernel, scale), out_shape=jax.Shape...  79.5 us
    unnamed x1, local copies, waits for them, and re-layouts  1.7 us

profile of v5, /device:TPU:40, one launch (start us, length us, event | category | flops | bytes accessed | tf_op | source)
XLA Modules:
  0.0 82.9 jit_solution(11388028747242422998)
XLA Ops:
  0.0 1.7 %copy.9 = bf16[48,3,2,1,512]{4,0,2,1,3:T(8,128)(2,1)} copy(bf16[48,3,2,1,512]{4,2,3,1,0:T(2,128)(2,1)} %param.6) | data formatting | bytes 589824 | tf_op args[0]
  1.7 79.5 %shard_map.64 = f32[144,128]{1,0:T(8,128)} custom-call(s32[3]{0:T(128)} %weights.1, s32[2,3]{1,0:T(2,128)} %bitcast.12, s32[3]{0:T(128)} %moms.1, bf16[6,48,512]{2,1,0:T(8,128)(2,1)} %bitcast.9, f32[54,1,512]{2,1,0:T(1,128)} %bitcast.11, f32[4,4,2,96,96]{4,3,2,1,0:T(8,128)} %peram.1), custom_call_target="tpu_custom_call" | custom-call | tf_op jit(solution)/shard_map/pallas_call | solution.py:549
  81.2 1.6 %copy.10 = f32[144,96]{0,1:T(8,128)} copy(f32[144,96]{1,0:T(8,128)} %bitcast.10) | data formatting | bytes 110592 | tf_op jit(solution)/shard_map/slice | solution.py:596
